TPU v7x, 32 devices: a whole 2x2x4 slice. The times are simulated.
32 devices in a mesh: rep: 2 (over y), seq: 4 (over z), tp: 4 (over x, core).
Axes of the slice: x: 2, y: 2, z: 4, core: 2. Of those that a mesh axis runs over, the one named last changes fastest.
Arguments:
- queries: bfloat16 [128, 64, 128], P(('rep', 'seq')), parts along dimension 0, may hold values from -9 to 9
- key_pages: bfloat16 [1024, 8, 64, 128], P(('rep', 'seq'), 'tp'), parts along dimension 0, may hold values from -4 to 4
- value_pages: bfloat16 [1024, 8, 64, 128], P(('rep', 'seq'), 'tp'), parts along dimension 0, may hold values from -6 to 6
- page_owner: int32 [128, 128], P('rep'), parts along dimension 0, may hold values from 0 to 3, as said below
- page_local: int32 [128, 128], P('rep'), parts along dimension 0, may hold values from 0 to 127, as said below
- seq_lengths: int32 [128], P('rep'), parts along dimension 0, may hold values from 1 to 8192, as said below
Outputs:
- attention: bfloat16 [128, 64, 128], P(('rep', 'seq'), 'tp'), parts along dimension 0
There are 2 independent parts, one for each index of `rep`. A program takes and returns all parts, laid end to end along the dimension named above; each array names one. Nothing has to cross between parts.
Inputs may be any that keep to these rules, and one draw needn't show every extreme that they name: The live slots (s * 64 < seq_lengths[b]) name pairs (page_owner, page_local) that are all different; the other slots hold 0. `page_local`: see page_owner. `seq_lengths`: one sequence has exactly 8192 tokens; the live slots of all sequences together number at most half of the 512 pages.
All inputs are finite; a program needn't handle non-finite values.
Results may differ from a plain program's by a relative error of at most 0.008.
Values may be sent and summed in bfloat16 or wider, within the bound.
A program may use at most 64 MiB of HBM per device.

v0:
```python
import math
import jax
import jax.numpy as jnp
from jax import lax
from jax.sharding import PartitionSpec as P

HQ = 64
KVH = 8
score_shift = 8.0


def body(queries, key_pages, value_pages, page_owner, page_local, seq_lengths):
    seq_count = page_owner.shape[0]
    slot_count = page_owner.shape[1]
    pool_pages = key_pages.shape[0]
    kv_local = key_pages.shape[1]
    page_len = key_pages.shape[2]
    head_dim = key_pages.shape[3]
    group_size = HQ // KVH
    heads_local = kv_local * group_size
    seq_rank = lax.axis_index("seq")
    tp_rank = lax.axis_index("tp")
    slot_ids = jnp.arange(slot_count, dtype=jnp.int32)
    slot_fill = jnp.clip(seq_lengths[:, None] - slot_ids[None, :] * page_len, 0, page_len)
    owned = (slot_fill > 0) & (page_owner == seq_rank)
    pool_range = jnp.arange(pool_pages, dtype=jnp.int32)
    matches = ((page_local[:, :, None] == pool_range[None, None, :]) & owned[:, :, None]).astype(
        jnp.bfloat16
    )
    fill_weight = slot_fill.astype(jnp.bfloat16)
    fill_table = jnp.einsum("bsp,bs->bp", matches, fill_weight, preferred_element_type=jnp.float32)
    hit_table = jnp.sum(matches.astype(jnp.float32), axis=1)
    seq_weight = jnp.arange(seq_count, dtype=jnp.float32)
    page_seq = jnp.dot(seq_weight, hit_table, precision=lax.Precision.HIGHEST).astype(jnp.int32)
    page_fill = jnp.sum(fill_table, axis=0).astype(jnp.int32)
    local_heads = lax.dynamic_slice_in_dim(queries, tp_rank * heads_local, heads_local, 1)
    head_queries = lax.all_gather(local_heads, "seq", axis=0, tiled=True)
    query_flat = head_queries.reshape(seq_count, heads_local * head_dim)
    score_scale = 1.0 / math.sqrt(head_dim)
    seq_range = jnp.arange(seq_count, dtype=jnp.int32)
    count = page_seq.shape[0]
    selector = page_seq[:, None] == seq_range[None, :]
    picked = jnp.dot(
        selector.astype(jnp.bfloat16), query_flat, preferred_element_type=jnp.float32
    ).astype(jnp.bfloat16)
    picked = picked.reshape(count, kv_local, group_size, head_dim)
    scores = (
        jnp.einsum("pkgd,pktd->pkgt", picked, key_pages, preferred_element_type=jnp.float32)
        * score_scale
    )
    live_mask = jnp.arange(page_len, dtype=jnp.int32)[None, :] < page_fill[:, None]
    weight = jnp.where(live_mask[:, None, None, :], jnp.exp(scores - score_shift), 0.0)
    page_total = jnp.sum(weight, axis=-1)
    page_sum = jnp.einsum(
        "pkgt,pktd->pkgd",
        weight.astype(jnp.bfloat16),
        value_pages,
        preferred_element_type=jnp.float32,
    )
    spread = selector.astype(jnp.float32).T
    numerator = jnp.dot(
        spread, page_sum.reshape(count, heads_local * head_dim), precision=lax.Precision.HIGHEST
    )
    denominator = jnp.dot(
        spread, page_total.reshape(count, heads_local), precision=lax.Precision.HIGHEST
    )
    numerator, denominator = (numerator, denominator)
    own_rows = seq_count // lax.axis_size("seq")
    summed_num, summed_den = lax.psum((numerator, denominator), "seq")
    summed_num = lax.dynamic_slice_in_dim(summed_num, seq_rank * own_rows, own_rows, 0)
    summed_den = lax.dynamic_slice_in_dim(summed_den, seq_rank * own_rows, own_rows, 0)
    result = summed_num.reshape(own_rows, heads_local, head_dim) / summed_den[..., None]
    return result.astype(jnp.bfloat16)


def solution(mesh):
    placed = (
        P(("rep", "seq"), None, None),
        P(("rep", "seq"), "tp", None, None),
        P(("rep", "seq"), "tp", None, None),
        P("rep", None),
        P("rep", None),
        P("rep"),
    )
    return jax.shard_map(
        body, mesh=mesh, in_specs=placed, out_specs=P(("rep", "seq"), "tp", None), check_vma=False
    )
```

profile of v0, /device:TPU:0, one launch (start us, length us, event | category | flops | bytes accessed | tf_op | source)
XLA Modules:
  0.0 89.1 jit_solution(877653192962036179)
XLA Ops:
  6.5 0.0 copy-start
  6.5 0.0 all-reduce.2.cloned.1.call-start
  6.5 0.8 fusion.35
  7.3 0.8 fusion.34
  8.2 4.5 %convert_reduce_fusion = f32[64,128]{1,0:T(8,128)S(1)} fusion(s32[64,128]{1,0:T(8,128)} %param.10, pred[64,128]{1,0:T(8,128)(4,1)S(1)} %fusion.34), kind=kLoop, calls=%fused_computation | loop fusion | flops 5234688 | bytes 73728 | tf_op jit(solution)/shard_map/reduce_sum | solution.py:32
  12.7 3.1 %fusion.14 = s32[128]{0:T(128)S(1)} fusion(s32[64,128]{1,0:T(8,128)} %param.10, pred[64,128]{1,0:T(8,128)(4,1)S(1)} %fusion.34, bf16[64,128,1]{1,0,2:T(8,128)(2,1)S(1)} %fusion.35), kind=kOutput, calls=%fused_computation.16 | convolution fusion | flops 4194432 | bytes 57856 | tf_op jit(solution)/shard_map/bsp,bs->bp/dot_general | solution.py:31
  15.8 0.1 iota_compare_fusion.1
  15.9 0.1 fusion.10
  16.0 0.0 copy-done
  16.0 0.0 copy-start.1
  16.1 15.8 %all_gather.3 = bf16[64,16,128]{2,1,0:T(8,128)(2,1)S(1)} all-gather(bf16[16,16,128]{2,1,0:T(8,128)(2,1)S(1)} %constant_dynamic-slice_fusion.1), channel_id=1, replica_groups=mesh['rep'=2,'seq'=4,'tp'=4] {'seq'}, dimensions={0}, use_global_device_ids=true | all-gather | bytes 327680 | tf_op jit(solution)/shard_map/all_gather | solution.py:37
  31.9 0.3 fusion.9
  32.2 0.1 copy.11
  32.3 4.6 %fusion.38 = (f32[128,2,8]{2,1,0:T(2,128)S(1)}, bf16[128,2,8,64]{3,2,1,0:T(8,128)(2,1)S(1)}) fusion(bf16[128,2,8,128]{3,2,1,0:T(8,128)(2,1)S(1)} %bitcast.38, bf16[128,2,64,128]{3,2,1,0:T(8,128)(2,1)} %param.7, pred[128,64]{1,0:T(8,128)(4,1)S(1)} %iota_compare_fusion.1), kind=kOutput, calls=%fused_computation.45 | convolution fusion | flops 34207744 | bytes 4997120 | tf_op jit(solution)/shard_map/pkgd,pktd->pkgt/dot_general | solution.py:48
  37.0 0.0 copy-done.1
  37.0 1.2 %fusion.20 = f32[128,2,8,128]{3,2,1,0:T(8,128)S(1)} fusion(bf16[128,2,64,128]{3,2,1,0:T(8,128)(2,1)S(1)} %copy-done.1, bf16[128,2,8,64]{3,2,1,0:T(8,128)(2,1)S(1)} %get-tuple-element.6), kind=kOutput, calls=%fused_computation.20 | convolution fusion | flops 33554432 | bytes 5505024 | tf_op jit(solution)/shard_map/pkgt,pktd->pkgd/dot_general | solution.py:54
  38.2 1.7 %fusion.17 = f32[64,2048]{1,0:T(8,128)} fusion(f32[16,8,16,128]{3,2,1,0:T(8,128)S(1)} %bitcast.37, s32[128]{0:T(128)S(1)} %fusion.10), kind=kOutput, calls=%fused_computation.17 | convolution fusion | flops 201334784 | bytes 1573376 | tf_op jit(solution)/shard_map/dot_general | solution.py:61
  39.8 0.0 all-reduce.2.cloned.1.call-update
  39.8 0.1 copy.8
  39.9 0.3 fusion.26
  40.2 20.0 %psum.15 = f32[64,16]{1,0:T(8,128)S(1)} all-reduce(f32[64,16]{1,0:T(8,128)S(1)} %fusion.26), channel_id=1, replica_groups=mesh['rep'=2,'seq'=4,'tp'=4] {'seq'}, use_global_device_ids=true, to_apply=%region_3.4 | all-reduce | flops 1024 | bytes 8192 | tf_op jit(solution)/shard_map/psum | solution.py:69
  60.2 20.3 %all-reduce.2.cloned.1.call-done = f32[64,2048]{1,0:T(8,128)} async-done(((f32[64,2048]{1,0:T(8,128)}), f32[64,2048]{1,0:T(8,128)}) %all-reduce.2.cloned.1.call-update) | async-done | bytes 524304 | tf_op jit(solution)/shard_map/psum | solution.py:69
  80.6 0.9 %dynamic-slice_bitcast_fusion = f32[2,8,16,128]{3,1,2,0:T(8,128)S(1)} fusion(f32[64,2048]{1,0:T(8,128)} %all-reduce.2.cloned.1.call-done, s32[]{:T(128)S(6)} %select_n.13), kind=kLoop, calls=%fused_computation.26 | loop fusion | bytes 262148
  81.5 0.7 fusion.24
  (4 shorter events, 0.1 us)
Async XLA Ops:
  6.5 9.5 %copy-start = (bf16[16,64,128]{2,1,0:T(8,128)(2,1)S(1)}, bf16[16,64,128]{2,1,0:T(8,128)(2,1)}, u32[]{:S(2)}) copy-start(bf16[16,64,128]{2,1,0:T(8,128)(2,1)} %param.6) | copy-start | bytes 786436
  6.5 74.0 %all-reduce.2.cloned.1.call-start = ((), (), s32[]{:S(2)}) async-start(), calls=%async_computation | async-start | bytes 1048576 | tf_op jit(solution)/shard_map/psum | solution.py:69
  16.0 20.9 %copy-start.1 = (bf16[128,2,64,128]{3,2,1,0:T(8,128)(2,1)S(1)}, bf16[128,2,64,128]{3,2,1,0:T(8,128)(2,1)}, u32[]{:S(2)}) copy-start(bf16[128,2,64,128]{3,2,1,0:T(8,128)(2,1)} %param.8) | copy-start | bytes 12582916
Sparse Core Ops, SparseCore 0:
  40.0 40.5 all-reduce.1
where the time goes:
time: 89.6 us; the launch traced here: 89.1 us
  blocking collectives  35.8 us (40%)
  waiting for transfers between devices  20.3 us (23%)
  between operations  13.5 us (15%)
  matrix products  11.4 us (13%)
  other arithmetic  6.96 us (8%)
  local copies, waits for them, and re-layouts  1.15 us (1%)
    psum x1, waiting for transfers between devices, body(): summed_num, summed_den = lax.psum((numerator, denominator), 'seq')  20.3 us
    psum x1, blocking collectives, body(): summed_num, summed_den = lax.psum((numerator, denominator), 'seq')  20 us
    all_gather x1, blocking collectives, body(): head_queries = lax.all_gather(local_heads, 'seq', axis=0, tiled=True)  15.8 us
    dot_general x1, matrix products, body(): jnp.einsum('pkgd,pktd->pkgt', picked, key_pages, preferred_element_type=j...  4.63 us
    reduce_sum x1, other arithmetic, body(): hit_table = jnp.sum(matches.astype(jnp.float32), axis=1)  4.51 us
    dot_general x1, matrix products, body(): jnp.einsum('bsp,bs->bp', matches, fill_weight, preferred_element_type=jnp...  3.1 us
  transfers between devices with their start and end apart: 1, of which 1 were waited for; matrix products, arithmetic and copies ran while one was open for 0% of the time, Pallas kernels for 0%

commit v1 on v0

--- a/solution.py
+++ b/solution.py
@@ -34,7 +34,12 @@
     page_seq = jnp.dot(seq_weight, hit_table, precision=lax.Precision.HIGHEST).astype(jnp.int32)
     page_fill = jnp.sum(fill_table, axis=0).astype(jnp.int32)
     local_heads = lax.dynamic_slice_in_dim(queries, tp_rank * heads_local, heads_local, 1)
-    head_queries = lax.all_gather(local_heads, "seq", axis=0, tiled=True)
+    ring = [local_heads]
+    for hop in range(3):
+        ring.append(lax.ppermute(ring[-1], "seq", [(dev, (dev + 1) % 4) for dev in range(4)]))
+    head_queries = jnp.roll(
+        jnp.concatenate(ring[::-1], axis=0), (lax.axis_index("seq") + 1) * ring[0].shape[0], axis=0
+    )
     query_flat = head_queries.reshape(seq_count, heads_local * head_dim)
     score_scale = 1.0 / math.sqrt(head_dim)
     seq_range = jnp.arange(seq_count, dtype=jnp.int32)

time: 89.6 us -> 88.4 us (0.987)
  blocking collectives: 35.8 us -> 16.1 us
  waiting for transfers between devices: 20.3 us -> 31.1 us
  starting transfers between devices: 0.01 us -> 4.69 us
  local copies, waits for them, and re-layouts: 1.15 us -> 4.16 us
    all_gather x1 -> x0, blocking collectives: 15.8 us -> none  [body(): head_queries = lax.all_gather(local_heads, 'seq', axis=0, tiled=True)]
    ppermute x0 -> x3, waiting for transfers between devices: none -> 10.3 us  [body(): lax.ppermute(ring[-1], 'seq', [(dev, (dev + 1) % 4) for dev in range(4)])]
    ppermute x0 -> x3, starting transfers between devices: none -> 4.68 us  [body(): lax.ppermute(ring[-1], 'seq', [(dev, (dev + 1) % 4) for dev in range(4)])]
    psum x1, blocking collectives: 20 us -> 16.1 us  [body(): summed_num, summed_den = lax.psum((numerator, denominator), 'seq')]
    unnamed x7 -> x12, local copies, waits for them, and re-layouts: 1.06 us -> 2.15 us
    concatenate x0 -> x1, local copies, waits for them, and re-layouts: none -> 1.07 us  [body(): jnp.roll(jnp.concatenate(ring[::-1], axis=0), (lax.axis_index('seq') + 1)...]
  transfers between devices with their start and end apart: 1 -> 4, of which waited for: 1 -> 3; matrix products, arithmetic and copies ran while one was open for 0% -> 11% of each run, Pallas kernels for 0% -> 0%
where the time goes in v1:
time: 88.4 us; the launch traced here: 87.8 us
  waiting for transfers between devices  31.1 us (35%)
  blocking collectives  16.1 us (18%)
  between operations  13.6 us (15%)
  matrix products  11.4 us (13%)
  other arithmetic  6.9 us (8%)
  starting transfers between devices  4.69 us (5%)
  local copies, waits for them, and re-layouts  4.16 us (5%)
    psum x1, waiting for transfers between devices, body(): summed_num, summed_den = lax.psum((numerator, denominator), 'seq')  20.7 us
    psum x1, blocking collectives, body(): summed_num, summed_den = lax.psum((numerator, denominator), 'seq')  16.1 us
    ppermute x3, waiting for transfers between devices, body(): lax.ppermute(ring[-1], 'seq', [(dev, (dev + 1) % 4) for dev in range(4)])  10.3 us
    ppermute x3, starting transfers between devices, body(): lax.ppermute(ring[-1], 'seq', [(dev, (dev + 1) % 4) for dev in range(4)])  4.68 us
    dot_general x1, matrix products, body(): jnp.einsum('pkgd,pktd->pkgt', picked, key_pages, preferred_element_type=j...  4.63 us
    reduce_sum x1, other arithmetic, body(): hit_table = jnp.sum(matches.astype(jnp.float32), axis=1)  4.51 us
    dot_general x1, matrix products, body(): jnp.einsum('bsp,bs->bp', matches, fill_weight, preferred_element_type=jnp...  3.1 us
    unnamed x12, local copies, waits for them, and re-layouts  2.15 us
  transfers between devices with their start and end apart: 4, of which 3 were waited for; matrix products, arithmetic and copies ran while one was open for 11% of the time, Pallas kernels for 0%

profile of v1, /device:TPU:0, one launch (start us, length us, event | category | flops | bytes accessed | tf_op | source)
XLA Modules:
  0.0 87.8 jit_solution(15224476766246300852)
XLA Ops:
  6.5 0.8 constant_dynamic-slice_fusion.2
  7.4 3.1 %collective-permute-start = (bf16[16,16,128]{2,1,0:T(8,128)(2,1)S(1)}, bf16[16,16,128]{2,1,0:T(8,128)(2,1)S(1)}, u32[]{:S(2)}, u32[]{:S(2)}) collective-permute-start(bf16[16,16,128]{2,1,0:T(8,128)(2,1)S(1)} %constant_dynamic-slice_fusion.2), channel_id=1, source_target_pairs={{0,4},{4,8},{8,12},{12,0},{1,5},{5,9},{9,13},{13,1},{2,6},{6,10},{... | collective-permute-start | bytes 196616 | tf_op jit(solution)/shard_map/ppermute | solution.py:39
  10.4 0.7 fusion.35
  11.2 0.8 fusion.34
  12.0 3.1 %fusion.14 = s32[128]{0:T(128)S(1)} fusion(s32[64,128]{1,0:T(8,128)} %param.10, pred[64,128]{1,0:T(8,128)(4,1)S(1)} %fusion.34, bf16[64,128,1]{1,0,2:T(8,128)(2,1)S(1)} %fusion.35), kind=kOutput, calls=%fused_computation.16 | convolution fusion | flops 4194432 | bytes 57856 | tf_op jit(solution)/shard_map/bsp,bs->bp/dot_general | solution.py:31
  15.1 4.5 %convert_reduce_fusion = f32[64,128]{1,0:T(8,128)S(1)} fusion(s32[64,128]{1,0:T(8,128)} %param.10, pred[64,128]{1,0:T(8,128)(4,1)S(1)} %fusion.34), kind=kLoop, calls=%fused_computation | loop fusion | flops 5234688 | bytes 73728 | tf_op jit(solution)/shard_map/reduce_sum | solution.py:32
  19.6 1.6 %collective-permute-start.1 = (bf16[16,16,128]{2,1,0:T(8,128)(2,1)S(1)}, bf16[16,16,128]{2,1,0:T(8,128)(2,1)S(1)}, u32[]{:S(2)}, u32[]{:S(2)}) collective-permute-start(bf16[16,16,128]{2,1,0:T(8,128)(2,1)S(1)} %collective-permute-done), channel_id=1, source_target_pairs={{0,4},{4,8},{8,12},{12,0},{1,5},{5,9},{9,13},{13,1},{2,6},{6,10},{... | collective-permute-start | bytes 196616 | tf_op jit(solution)/shard_map/ppermute | solution.py:39
  21.3 0.1 fusion.10
  21.4 4.3 %collective-permute-done.1 = bf16[16,16,128]{2,1,0:T(8,128)(2,1)S(1)} collective-permute-done((bf16[16,16,128]{2,1,0:T(8,128)(2,1)S(1)}, bf16[16,16,128]{2,1,0:T(8,128)(2,1)S(1)}, u32[]{:S(2)}, u32[]{:S(2)}) %collective-permute-start.1) | collective-permute-done | bytes 65568 | tf_op jit(solution)/shard_map/ppermute | solution.py:39
  25.8 0.1 iota_compare_fusion.1
  25.9 6.0 %collective-permute-done.2 = bf16[16,16,128]{2,1,0:T(8,128)(2,1)S(1)} collective-permute-done((bf16[16,16,128]{2,1,0:T(8,128)(2,1)S(1)}, bf16[16,16,128]{2,1,0:T(8,128)(2,1)S(1)}, u32[]{:S(2)}, u32[]{:S(2)}) %collective-permute-start.2) | collective-permute-done | bytes 65568 | tf_op jit(solution)/shard_map/ppermute | solution.py:39
  31.9 1.0 %constant_dynamic-update-slice_fusion.4 = bf16[128,16,128]{2,1,0:T(8,128)(2,1)S(1)} fusion(bf16[128,16,128]{2,1,0:T(8,128)(2,1)S(1)} %constant_dynamic-update-slice_fusion.5, bf16[16,64,128]{2,1,0:T(8,128)(2,1)} %param.6, s32[]{:T(128)S(6)} %select_n.24), kind=kLoop, calls=%fused_computation.43 | loop fusion | bytes 131076
  33.0 1.1 %constant_dynamic-update-slice_fusion = bf16[128,16,128]{2,1,0:T(8,128)(2,1)S(1)} fusion(bf16[128,16,128]{2,1,0:T(8,128)(2,1)S(1)} %constant_dynamic-update-slice_fusion.1, bf16[16,64,128]{2,1,0:T(8,128)(2,1)} %param.6, s32[]{:T(128)S(6)} %select_n.24), kind=kLoop, calls=%fused_computation.39 | loop fusion | bytes 131076 | tf_op jit(solution)/shard_map/jit(_roll_dynamic)/concatenate | solution.py:40
  34.1 0.3 fusion.9
  34.4 0.1 copy.11
  34.5 4.6 %fusion.38 = (f32[128,2,8]{2,1,0:T(2,128)S(1)}, bf16[128,2,8,64]{3,2,1,0:T(8,128)(2,1)S(1)}) fusion(bf16[128,2,8,128]{3,2,1,0:T(8,128)(2,1)S(1)} %bitcast.38, bf16[128,2,64,128]{3,2,1,0:T(8,128)(2,1)} %param.7, pred[128,64]{1,0:T(8,128)(4,1)S(1)} %iota_compare_fusion.1), kind=kOutput, calls=%fused_computation.54 | convolution fusion | flops 34207744 | bytes 4997120 | tf_op jit(solution)/shard_map/pkgd,pktd->pkgt/dot_general | solution.py:53
  39.2 1.2 %fusion.20 = f32[128,2,8,128]{3,2,1,0:T(8,128)S(1)} fusion(bf16[128,2,64,128]{3,2,1,0:T(8,128)(2,1)S(1)} %copy-done, bf16[128,2,8,64]{3,2,1,0:T(8,128)(2,1)S(1)} %get-tuple-element.6), kind=kOutput, calls=%fused_computation.20 | convolution fusion | flops 33554432 | bytes 5505024 | tf_op jit(solution)/shard_map/pkgt,pktd->pkgd/dot_general | solution.py:59
  40.4 1.7 %fusion.17 = f32[64,2048]{1,0:T(8,128)} fusion(f32[16,8,16,128]{3,2,1,0:T(8,128)S(1)} %bitcast.37, s32[128]{0:T(128)S(1)} %fusion.10), kind=kOutput, calls=%fused_computation.17 | convolution fusion | flops 201334784 | bytes 1573376 | tf_op jit(solution)/shard_map/dot_general | solution.py:66
  42.0 0.1 copy.8
  42.1 0.3 fusion.26
  42.4 16.1 %psum.15 = f32[64,16]{1,0:T(8,128)S(1)} all-reduce(f32[64,16]{1,0:T(8,128)S(1)} %fusion.26), channel_id=1, replica_groups=mesh['rep'=2,'seq'=4,'tp'=4] {'seq'}, use_global_device_ids=true, to_apply=%region_3.4 | all-reduce | flops 1024 | bytes 8192 | tf_op jit(solution)/shard_map/psum | solution.py:74
  58.6 20.7 %all-reduce.2.cloned.1.call-done = f32[64,2048]{1,0:T(8,128)} async-done(((f32[64,2048]{1,0:T(8,128)}), f32[64,2048]{1,0:T(8,128)}) %all-reduce.2.cloned.1.call-update) | async-done | bytes 524304 | tf_op jit(solution)/shard_map/psum | solution.py:74
  79.3 0.9 %dynamic-slice_bitcast_fusion = f32[2,8,16,128]{3,1,2,0:T(8,128)S(1)} fusion(f32[64,2048]{1,0:T(8,128)} %all-reduce.2.cloned.1.call-done, s32[]{:T(128)S(6)} %select_n.28), kind=kLoop, calls=%fused_computation.26 | loop fusion | bytes 262148
  80.2 0.7 fusion.24
  (16 shorter events, 0.2 us)
Async XLA Ops:
  6.5 72.8 %all-reduce.2.cloned.1.call-start = ((), (), s32[]{:S(2)}) async-start(), calls=%async_computation | async-start | bytes 1048576 | tf_op jit(solution)/shard_map/psum | solution.py:74
  7.4 12.3 %collective-permute-start = (bf16[16,16,128]{2,1,0:T(8,128)(2,1)S(1)}, bf16[16,16,128]{2,1,0:T(8,128)(2,1)S(1)}, u32[]{:S(2)}, u32[]{:S(2)}) collective-permute-start(bf16[16,16,128]{2,1,0:T(8,128)(2,1)S(1)} %constant_dynamic-slice_fusion.2), channel_id=1, source_target_pairs={{0,4},{4,8},{8,12},{12,0},{1,5},{5,9},{9,13},{13,1},{2,6},{6,10},{... | collective-permute-start | bytes 196616 | tf_op jit(solution)/shard_map/ppermute | solution.py:39
  19.6 6.1 %collective-permute-start.1 = (bf16[16,16,128]{2,1,0:T(8,128)(2,1)S(1)}, bf16[16,16,128]{2,1,0:T(8,128)(2,1)S(1)}, u32[]{:S(2)}, u32[]{:S(2)}) collective-permute-start(bf16[16,16,128]{2,1,0:T(8,128)(2,1)S(1)} %collective-permute-done), channel_id=1, source_target_pairs={{0,4},{4,8},{8,12},{12,0},{1,5},{5,9},{9,13},{13,1},{2,6},{6,10},{... | collective-permute-start | bytes 196616 | tf_op jit(solution)/shard_map/ppermute | solution.py:39
  25.8 6.1 %collective-permute-start.2 = (bf16[16,16,128]{2,1,0:T(8,128)(2,1)S(1)}, bf16[16,16,128]{2,1,0:T(8,128)(2,1)S(1)}, u32[]{:S(2)}, u32[]{:S(2)}) collective-permute-start(bf16[16,16,128]{2,1,0:T(8,128)(2,1)S(1)} %collective-permute-done.1), channel_id=1, source_target_pairs={{0,4},{4,8},{8,12},{12,0},{1,5},{5,9},{9,13},{13,1},{2,6},{6,10},{... | collective-permute-start | bytes 196616 | tf_op jit(solution)/shard_map/ppermute | solution.py:39
  31.9 7.3 %copy-start = (bf16[128,2,64,128]{3,2,1,0:T(8,128)(2,1)S(1)}, bf16[128,2,64,128]{3,2,1,0:T(8,128)(2,1)}, u32[]{:S(2)}) copy-start(bf16[128,2,64,128]{3,2,1,0:T(8,128)(2,1)} %param.8) | copy-start | bytes 12582916
Sparse Core Ops, SparseCore 0:
  42.2 37.0 all-reduce.1
